TPU v7x, 256 devices: a whole 4x4x8 slice. The times are simulated.
256 devices in a mesh: obs: 64 (over z, y, core), rep: 4 (over x).
Axes of the slice: x: 4, y: 4, z: 8, core: 2. Of those that a mesh axis runs over, the one named last changes fastest.
Arguments:
- jacobians: float32 [18, 8388608], P(None, ('obs', 'rep')), may hold values from -3 to 3
- residuals: float32 [2, 8388608], P(None, ('obs', 'rep')), may hold values from -6 to 6
- camera_local: int32 [8388608], P(('obs', 'rep')), may hold values from 0 to 1023
- bucket_counts: int32 [256, 64], P(('obs', 'rep')), may hold values from 1 to 512, as said below
- camera_map: int32 [65536], replicated, may hold values from 0 to 65535, each once
Outputs:
- gradient: float32 [9, 65536], replicated
- camera_blocks: float32 [81, 65536], P(None, 'obs')
Inputs may be any that keep to these rules, and one draw needn't show every extreme that they name: bucket_counts[s, d] counts the leading live slots of bucket d of source block s; exactly one destination d has all 512 slots live from every source block, and every other bucket has at most 256 live slots. A slot in bucket d names camera slot d * 1024 + camera_local. `camera_map`: each camera id appears once.
All inputs are finite; a program needn't handle non-finite values.
Results may differ from a plain program's by a relative error of at most 0.0003.
Values sent between devices are 32-bit elements; how exact they have to be, the bound alone decides.
A program may use at most 192 MiB of HBM per device.

v0:
```python
import math
import jax
import jax.numpy as jnp
from jax import lax
from jax.sharding import Mesh
from jax.sharding import PartitionSpec as P

CAM_DEV = 1024
OBS = ("obs_0", "obs_1", "obs_2")
OBS_REP = ("obs_0", "obs_1", "obs_2", "rep")


def sent_together(arrays, axis, split_dim, concat_dim, along):
    widths = [a.shape[along] for a in arrays]
    both = jnp.concatenate(arrays, axis=along)
    filled = lax.all_to_all(both, axis, split_axis=split_dim, concat_axis=concat_dim, tiled=True)
    return tuple(jnp.split(filled, [sum(widths[:k]) for k in range(1, len(widths))], axis=along))


def split_up(shard, dim, count):
    shape = shard.shape
    pieces = shard.reshape(*shape[:dim], count, shape[dim] // count, *shape[dim + 1 :])
    return jnp.moveaxis(pieces, dim, 0)


def summed_on_arrival(shard, axis, dim):
    pieces = split_up(shard, dim, lax.axis_size(axis))
    arrived = lax.all_to_all(pieces, axis, split_axis=0, concat_axis=0, tiled=True)
    return arrived.sum(axis=0)


def side_by_side(arrays, axis, dim, along):
    both = jnp.concatenate(arrays, axis=along)
    filled, at, finished = (summed_on_arrival(both, axis, dim), 0, [])
    for a in arrays:
        finished.append(lax.slice_in_dim(filled, at, at + a.shape[along], axis=along))
        at += a.shape[along]
    return tuple(finished)


def in_order(pieces, dim):
    shape = list(pieces.shape[1:])
    shape[dim] *= pieces.shape[0]
    return jnp.moveaxis(pieces, 0, dim).reshape(shape)


def stacked_from(shard, axes, order):
    pieces = shard[None]
    for k in order:
        pieces = lax.all_gather(pieces, axes[k], axis=0, tiled=True)
    carried = [lax.axis_size(axes[k]) for k in reversed(order)]
    pieces = pieces.reshape(*carried, *shard.shape)
    turned = sorted(range(len(order)), key=lambda place: order[len(order) - 1 - place])
    return pieces.transpose(*turned, *range(len(order), pieces.ndim)).reshape(-1, *shard.shape)


def whole_of(shard, axes, order, dim):
    return in_order(stacked_from(shard, axes, order), dim)


def sent_to_all(shard, axis):
    count = lax.axis_size(axis)
    return lax.all_to_all(
        jnp.broadcast_to(shard[None], (count, *shard.shape)), axis, 0, 0, tiled=True
    )


def gather_directly(shard, axis, dim):
    return in_order(sent_to_all(shard, axis), dim)


def observation_terms(jacobs, resids):
    leading_row = jacobs[0:9]
    trailing_row = jacobs[9:18]
    gradient_terms = leading_row * resids[0:1] + trailing_row * resids[1:2]
    block_terms = (
        leading_row[:, None] * leading_row[None, :] + trailing_row[:, None] * trailing_row[None, :]
    )
    block_terms = block_terms.reshape((81,) + leading_row.shape[1:])
    return jnp.concatenate([gradient_terms, block_terms], axis=0)


def grouped_sums(jac_flat, res_flat, ids_flat, live_flat, width):
    total = jac_flat.shape[1]
    groups = total // width
    camera_rows = lax.broadcasted_iota(jnp.int32, (CAM_DEV, 1), 0)

    def add_group(index, summed):
        start = index * width
        jac_piece = lax.dynamic_slice_in_dim(jac_flat, start, width, 1)
        res_piece = lax.dynamic_slice_in_dim(res_flat, start, width, 1)
        id_piece = lax.dynamic_slice_in_dim(ids_flat, start, width, 0)
        live_piece = lax.dynamic_slice_in_dim(live_flat, start, width, 0)[None, :]
        terms = observation_terms(jac_piece * live_piece, res_piece * live_piece)
        one_hot = (id_piece[None, :] == camera_rows).astype(jnp.float32)
        added = lax.dot_general(
            terms,
            one_hot,
            (((1,), (1,)), ((), ())),
            precision=lax.Precision.HIGHEST,
            preferred_element_type=jnp.float32,
        )
        return summed + added

    return lax.fori_loop(0, groups, add_group, jnp.zeros((90, CAM_DEV), jnp.float32))


def group_width(senders, width):
    return math.gcd(senders, max(1, 2048 // width)) * width


def local(jacobians, residuals, camera_local, bucket_counts, camera_map):
    senders = lax.axis_size(OBS)
    capacity = jacobians.shape[1] // senders
    jac_split = jacobians.reshape(18, senders, capacity)
    res_split = residuals.reshape(2, senders, capacity)
    ids_split = camera_local.reshape(1, senders, capacity)
    counts_here = bucket_counts.reshape(1, senders, 1)
    moved_jac, moved_res = sent_together((jac_split, res_split), OBS, 1, 1, 0)
    moved_ids, moved_counts = sent_together((ids_split, counts_here), OBS, 1, 1, 2)
    within = lax.broadcasted_iota(jnp.int32, (1, senders, capacity), 2)
    live_mask = (within < moved_counts).astype(jnp.float32)
    summed = grouped_sums(
        moved_jac.reshape(18, senders * capacity),
        moved_res.reshape(2, senders * capacity),
        moved_ids.reshape(senders * capacity),
        live_mask.reshape(senders * capacity),
        group_width(senders, capacity),
    )
    grad_part = summed[:9]
    block_part = summed[9:]
    grad_share, block_share = side_by_side((grad_part, block_part), "rep", 1, 0)
    grad_slots = whole_of(grad_share, OBS_REP, (0, 1, 3, 2), 1)
    blocks_out = gather_directly(block_share, "rep", 1)
    gradient = (
        jnp.zeros(grad_slots.shape, jnp.float32)
        .at[:, camera_map]
        .set(grad_slots, unique_indices=True)
    )
    return (gradient, blocks_out)


def solution(mesh):
    split = Mesh(
        mesh.devices.reshape(8, 4, 2, mesh.shape["rep"]), ("obs_0", "obs_1", "obs_2", "rep")
    )
    return jax.shard_map(
        local,
        mesh=split,
        in_specs=(P(None, OBS_REP), P(None, OBS_REP), P(OBS_REP), P(OBS_REP, None), P()),
        out_specs=(P(), P(None, OBS)),
        check_vma=False,
    )
```

profile of v0, /device:TPU:1, one launch (start us, length us, event | category | flops | bytes accessed | tf_op | source)
XLA Modules:
  0.0 553.7 jit_solution(11730834584020948406)
XLA Ops:
  9.7 13.1 %all-to-all-start.1 = ((s32[1,64,513]{2,0,1:T(1,128)}), s32[1,64,513]{2,0,1:T(1,128)S(1)}, u32[]{:S(2)}, u32[]{:S(2)}) async-start(s32[1,64,513]{2,0,1:T(1,128)} %copy.22), calls=%async_computation.1 | async-start | bytes 327680 | tf_op jit(solution)/shard_map/all_to_all | solution.py:16
  34.5 6.9 %all-to-all-start = ((f32[20,64,512]{2,0,1:T(8,128)}), f32[20,64,512]{2,0,1:T(8,128)S(1)}, u32[]{:S(2)}, u32[]{:S(2)}) async-start(f32[20,64,512]{2,0,1:T(8,128)} %copy.19), calls=%async_computation | async-start | bytes 6291456 | tf_op jit(solution)/shard_map/all_to_all | solution.py:16
  43.8 70.0 %all-to-all-done = f32[20,64,512]{2,0,1:T(8,128)S(1)} async-done(((f32[20,64,512]{2,0,1:T(8,128)}), f32[20,64,512]{2,0,1:T(8,128)S(1)}, u32[]{:S(2)}, u32[]{:S(2)}) %all-to-all-start) | async-done | bytes 2621472 | tf_op jit(solution)/shard_map/all_to_all | solution.py:16
  119.3 118.1 %while.14 = (s32[]{:T(128)}, f32[90,1024]{1,0:T(8,128)}, f32[18,32768]{1,0:T(8,128)}, f32[32768]{0:T(1024)}, f32[2,32768]{1,0:T(2,128)S(1)}, /*index=5*/s32[3276...) while((s32[]{:T(128)}, f32[90,1024]{1,0:T(8,128)}, f32[18,32768]{1,0:T(8,128)}, ...), condition=%wide.region_1.0_spmd.clone, body=%wide.region_0.0_spmd.clone.sunk | while | flops 2267983872 | bytes 7364837 | solution.py:105
  121.4 4.6 fusion.17
  128.8 4.6 fusion.17
  136.1 4.6 fusion.17
  143.5 4.6 fusion.17
  150.9 4.6 fusion.17
  158.3 4.6 fusion.17
  165.6 4.6 fusion.17
  173.0 4.6 fusion.17
  209.9 4.6 fusion.17
  217.3 4.6 fusion.17
  238.6 10.0 %all_to_all.20 = f32[4,90,256]{2,1,0:T(8,128)S(1)} all-to-all(f32[4,90,256]{2,1,0:T(8,128)S(1)} %copy.23), channel_id=1, replica_groups=mesh['obs_0'=8,'obs_1'=4,'obs_2'=2,'rep'=4] {'rep'}, dimensions={0} | all-to-all | bytes 737280 | tf_op jit(solution)/shard_map/all_to_all | solution.py:28
  248.7 21.8 %all-gather.1 = f32[8,9,256]{2,1,0:T(8,128)S(1)} all-gather(f32[1,9,256]{2,1,0:T(8,128)S(1)} %slice_bitcast_fusion), channel_id=2, replica_groups=mesh['obs_0'=8,'obs_1'=4,'obs_2'=2,'rep'=4] {'obs_0'}, dimensions={0}, use_global_device_ids=true | all-gather | bytes 82944 | tf_op jit(solution)/shard_map/all_gather | solution.py:50
  270.6 10.2 %all_gather.13 = f32[32,9,256]{2,0,1:T(8,128)} all-gather(f32[8,9,256]{2,0,1:T(8,128)S(1)} %copy.24), channel_id=1, replica_groups=mesh['obs_0'=8,'obs_1'=4,'obs_2'=2,'rep'=4] {'obs_1'}, dimensions={0}, use_global_device_ids=true | all-gather | bytes 368640 | tf_op jit(solution)/shard_map/all_gather | solution.py:50
  280.8 28.4 %all-gather.5.cloned.1.call-done = f32[128,9,256]{2,0,1:T(8,128)} async-done(((f32[32,9,256]{2,0,1:T(8,128)}), f32[128,9,256]{2,0,1:T(8,128)}) %all-gather.5.cloned.1.call-update) | async-done | bytes 1179664 | tf_op jit(solution)/shard_map/all_gather | solution.py:50
  313.7 6.0 %all-to-all-done.3 = f32[4,81,256]{2,1,0:T(8,128)S(1)} async-done(((f32[4,81,256]{2,1,0:T(8,128)}), f32[4,81,256]{2,1,0:T(8,128)S(1)}, u32[]{:S(2)}, u32[]{:S(2)}) %all-to-all-start.3) | async-done | bytes 331808 | tf_op jit(solution)/shard_map/all_to_all | solution.py:63
  320.7 10.1 %all-gather.7.cloned.1.call-done = f32[256,9,256]{2,0,1:T(8,128)} async-done(((f32[128,9,256]{2,0,1:T(8,128)}), f32[256,9,256]{2,0,1:T(8,128)}) %all-gather.7.cloned.1.call-update) | async-done | bytes 2359312 | tf_op jit(solution)/shard_map/all_gather | solution.py:50
  330.8 4.6 copy.37
  338.1 16.6 %copy.29 = f32[9,256,256]{0,2,1:T(8,128)} copy(f32[9,256,256]{2,1,0:T(8,128)S(1)} %bitcast.45) | data formatting | bytes 4718592 | tf_op jit(solution)/shard_map/reshape | solution.py:44
  354.7 172.8 %scatter_custom_fusion = f32[9,65536]{0,1:T(8,128)} fusion(s32[65536]{0:T(1024)S(1)} %compare_select_fusion, f32[65536,9]{1,0:T(8,128)} %bitcast.41, f32[]{:T(128)} %constant.34.clone.1), kind=kCustom, calls=%fused_computation.14 | custom fusion | bytes 2359808 | tf_op jit(solution)/shard_map/scatter | solution.py:138
  527.5 19.4 %copy.28 = f32[9,65536]{1,0:T(8,128)} copy(f32[9,65536]{0,1:T(8,128)} %scatter_custom_fusion) | data formatting | bytes 4718592
  (243 shorter events, 102.7 us)
Async XLA Ops:
  9.7 24.8 %all-to-all-start.1 = ((s32[1,64,513]{2,0,1:T(1,128)}), s32[1,64,513]{2,0,1:T(1,128)S(1)}, u32[]{:S(2)}, u32[]{:S(2)}) async-start(s32[1,64,513]{2,0,1:T(1,128)} %copy.22), calls=%async_computation.1 | async-start | bytes 327680 | tf_op jit(solution)/shard_map/all_to_all | solution.py:16
  34.5 7.2 %copy-start = (s32[1,64,513]{2,0,1:T(1,128)}, s32[1,64,513]{2,0,1:T(1,128)S(1)}, u32[]{:S(2)}) copy-start(s32[1,64,513]{2,0,1:T(1,128)S(1)} %all-to-all-done.1) | copy-start | bytes 393988
  34.5 79.4 %all-to-all-start = ((f32[20,64,512]{2,0,1:T(8,128)}), f32[20,64,512]{2,0,1:T(8,128)S(1)}, u32[]{:S(2)}, u32[]{:S(2)}) async-start(f32[20,64,512]{2,0,1:T(8,128)} %copy.19), calls=%async_computation | async-start | bytes 6291456 | tf_op jit(solution)/shard_map/all_to_all | solution.py:16
  41.4 267.8 %all-gather.5.cloned.1.call-start = ((), (), s32[]{:S(2)}) async-start(), calls=%async_computation.4 | async-start | bytes 1474560 | tf_op jit(solution)/shard_map/all_gather | solution.py:50
  115.6 3.6 slice-start
  119.3 2.1 copy-start.1
  126.7 2.1 copy-start.1
  134.1 2.1 copy-start.1
  141.4 2.1 copy-start.1
  148.8 2.1 copy-start.1
  156.2 2.1 copy-start.1
  163.6 2.1 copy-start.1
  171.0 2.1 copy-start.1
  178.3 2.1 copy-start.1
  185.7 2.1 copy-start.1
  193.1 2.1 copy-start.1
  200.5 2.1 copy-start.1
  207.8 2.1 copy-start.1
  215.2 2.1 copy-start.1
  222.6 2.1 copy-start.1
  230.0 2.1 copy-start.1
  237.3 76.3 %copy-start.4 = (s32[65536]{0:T(1024)S(1)}, s32[65536]{0:T(1024)}, u32[]{:S(2)}) copy-start(s32[65536]{0:T(1024)} %param.11) | copy-start | bytes 786436
  280.8 50.0 %all-gather.7.cloned.1.call-start = ((), (), s32[]{:S(2)}) async-start(), calls=%async_computation.5 | async-start | bytes 3538944 | tf_op jit(solution)/shard_map/all_gather | solution.py:50
  310.0 9.7 %all-to-all-start.3 = ((f32[4,81,256]{2,1,0:T(8,128)}), f32[4,81,256]{2,1,0:T(8,128)S(1)}, u32[]{:S(2)}, u32[]{:S(2)}) async-start(f32[4,81,256]{2,1,0:T(8,128)} %broadcast_in_dim.40), calls=%async_computation.3 | async-start | bytes 720896 | tf_op jit(solution)/shard_map/all_to_all | solution.py:63
  (17 other events, 12.8 us)
Sparse Core Ops, SparseCore 0:
  280.9 28.2 all-gather.4
  311.0 19.7 all-gather.6
where the time goes:
time: 555 us; the launch traced here: 554 us
  local copies, waits for them, and re-layouts  262 us (47%)
  waiting for transfers between devices  118 us (21%)
  matrix products  72.9 us (13%)
  blocking collectives  42 us (8%)
  starting transfers between devices  24 us (4%)
  other arithmetic  19.5 us (4%)
  between operations  14.2 us (3%)
    scatter x1, local copies, waits for them, and re-layouts, local(): gradient = jnp.zeros(grad_slots.shape, jnp.float32).at[:, camera_map].set...  173 us
    all_to_all x2, waiting for transfers between devices, sent_together(): lax.all_to_all(both, axis, split_axis=split_dim, concat_axis=concat_dim,...  73.4 us
    dot_general x16, matrix products, add_group(): lax.dot_general(terms, one_hot, (((1,), (1,)), ((), ())), precision=lax.P...  72.9 us
    all_gather x2, waiting for transfers between devices, stacked_from(): pieces = lax.all_gather(pieces, axes[k], axis=0, tiled=True)  38.4 us
    all_gather x2, blocking collectives, stacked_from(): pieces = lax.all_gather(pieces, axes[k], axis=0, tiled=True)  32 us
    unnamed x16, local copies, waits for them, and re-layouts  28.7 us
    all_to_all x2, starting transfers between devices, sent_together(): lax.all_to_all(both, axis, split_axis=split_dim, concat_axis=concat_dim,...  20.1 us
    reshape x1, local copies, waits for them, and re-layouts, in_order(): return jnp.moveaxis(pieces, 0, dim).reshape(shape)  16.6 us
  transfers between devices with their start and end apart: 5, of which 5 were waited for; matrix products, arithmetic and copies ran while one was open for 2% of the time, Pallas kernels for 0%

commit v1 on v0

--- a/solution.py
+++ b/solution.py
@@ -47,7 +47,9 @@
 def stacked_from(shard, axes, order):
     pieces = shard[None]
     for k in order:
-        pieces = lax.all_gather(pieces, axes[k], axis=0, tiled=True)
+        pieces = jnp.concatenate(
+            lax.all_to_all(jnp.stack([pieces] * lax.axis_size(axes[k])), axes[k], 0, 0), axis=0
+        )
     carried = [lax.axis_size(axes[k]) for k in reversed(order)]
     pieces = pieces.reshape(*carried, *shard.shape)
     turned = sorted(range(len(order)), key=lambda place: order[len(order) - 1 - place])

time: 555 us -> 521 us (0.939)
  waiting for transfers between devices: 118 us -> 96.3 us
  between operations: 14.2 us -> 0.88 us
  blocking collectives: 42 us -> 35 us
  starting transfers between devices: 24 us -> 30.6 us
    all_gather x2 -> x0, waiting for transfers between devices: 38.4 us -> none  [stacked_from(): pieces = lax.all_gather(pieces, axes[k], axis=0, tiled=True)]
    all_gather x2 -> x0, blocking collectives: 32 us -> none  [stacked_from(): pieces = lax.all_gather(pieces, axes[k], axis=0, tiled=True)]
    all_to_all x0 -> x2, blocking collectives: none -> 24.9 us  [stacked_from(): lax.all_to_all(jnp.stack([pieces] * lax.axis_size(axes[k])), axes[k], 0, 0)]
    all_to_all x0 -> x2, waiting for transfers between devices: none -> 16.7 us  [stacked_from(): lax.all_to_all(jnp.stack([pieces] * lax.axis_size(axes[k])), axes[k], 0, 0)]
    all_to_all x0 -> x2, starting transfers between devices: none -> 6.98 us  [stacked_from(): lax.all_to_all(jnp.stack([pieces] * lax.axis_size(axes[k])), axes[k], 0, 0)]
    unnamed x16 -> x15, local copies, waits for them, and re-layouts: 28.7 us -> 28.7 us
where the time goes in v1:
time: 521 us; the launch traced here: 519 us
  local copies, waits for them, and re-layouts  262 us (50%)
  waiting for transfers between devices  96.3 us (18%)
  matrix products  72.9 us (14%)
  blocking collectives  35 us (7%)
  starting transfers between devices  30.6 us (6%)
  other arithmetic  19.8 us (4%)
    scatter x1, local copies, waits for them, and re-layouts, local(): gradient = jnp.zeros(grad_slots.shape, jnp.float32).at[:, camera_map].set...  173 us
    all_to_all x2, waiting for transfers between devices, sent_together(): lax.all_to_all(both, axis, split_axis=split_dim, concat_axis=concat_dim,...  73.6 us
    dot_general x16, matrix products, add_group(): lax.dot_general(terms, one_hot, (((1,), (1,)), ((), ())), precision=lax.P...  72.9 us
    unnamed x15, local copies, waits for them, and re-layouts  28.7 us
    all_to_all x2, blocking collectives, stacked_from(): lax.all_to_all(jnp.stack([pieces] * lax.axis_size(axes[k])), axes[k], 0, 0)  24.9 us
    all_to_all x2, starting transfers between devices, sent_together(): lax.all_to_all(both, axis, split_axis=split_dim, concat_axis=concat_dim,...  20.1 us
    reshape x1, local copies, waits for them, and re-layouts, in_order(): return jnp.moveaxis(pieces, 0, dim).reshape(shape)  16.8 us
    all_to_all x2, waiting for transfers between devices, stacked_from(): lax.all_to_all(jnp.stack([pieces] * lax.axis_size(axes[k])), axes[k], 0, 0)  16.7 us
  transfers between devices with their start and end apart: 5, of which 5 were waited for; matrix products, arithmetic and copies ran while one was open for 2% of the time, Pallas kernels for 0%

profile of v1, /device:TPU:1, one launch (start us, length us, event | category | flops | bytes accessed | tf_op | source)
XLA Modules:
  0.0 519.0 jit_solution(4445822576633463569)
XLA Ops:
  3.2 13.1 %all-to-all-start.1 = ((s32[1,64,513]{2,0,1:T(1,128)}), s32[1,64,513]{2,0,1:T(1,128)S(1)}, u32[]{:S(2)}, u32[]{:S(2)}) async-start(s32[1,64,513]{2,0,1:T(1,128)} %copy.48), calls=%async_computation.1 | async-start | bytes 327680 | tf_op jit(solution)/shard_map/all_to_all | solution.py:16
  28.0 6.9 %all-to-all-start = ((f32[20,64,512]{2,0,1:T(8,128)}), f32[20,64,512]{2,0,1:T(8,128)S(1)}, u32[]{:S(2)}, u32[]{:S(2)}) async-start(f32[20,64,512]{2,0,1:T(8,128)} %copy.45), calls=%async_computation | async-start | bytes 6291456 | tf_op jit(solution)/shard_map/all_to_all | solution.py:16
  37.1 70.3 %all-to-all-done = f32[20,64,512]{2,0,1:T(8,128)S(1)} async-done(((f32[20,64,512]{2,0,1:T(8,128)}), f32[20,64,512]{2,0,1:T(8,128)S(1)}, u32[]{:S(2)}, u32[]{:S(2)}) %all-to-all-start) | async-done | bytes 2621472 | tf_op jit(solution)/shard_map/all_to_all | solution.py:16
  112.8 118.1 %while.14 = (s32[]{:T(128)}, f32[90,1024]{1,0:T(8,128)}, f32[18,32768]{1,0:T(8,128)}, f32[32768]{0:T(1024)}, f32[2,32768]{1,0:T(2,128)S(1)}, /*index=5*/s32[3276...) while((s32[]{:T(128)}, f32[90,1024]{1,0:T(8,128)}, f32[18,32768]{1,0:T(8,128)}, ...), condition=%wide.region_1.0_spmd.clone, body=%wide.region_0.0_spmd.clone.sunk | while | flops 2267983872 | bytes 7364837 | solution.py:107
  114.9 4.6 fusion.17
  122.2 4.6 fusion.17
  129.6 4.6 fusion.17
  137.0 4.6 fusion.17
  144.4 4.6 fusion.17
  151.7 4.6 fusion.17
  159.1 4.6 fusion.17
  166.5 4.6 fusion.17
  173.9 4.6 fusion.17
  196.0 4.6 fusion.17
  203.4 4.6 fusion.17
  232.1 10.0 %all_to_all.40 = f32[4,90,256]{2,1,0:T(8,128)S(1)} all-to-all(f32[4,90,256]{2,1,0:T(8,128)S(1)} %copy.49), channel_id=1, replica_groups=mesh['obs_0'=8,'obs_1'=4,'obs_2'=2,'rep'=4] {'rep'}, dimensions={0} | all-to-all | bytes 737280 | tf_op jit(solution)/shard_map/all_to_all | solution.py:28
  242.2 14.2 %all_to_all.41 = f32[8,1,9,256]{3,1,2,0:T(1,128)S(1)} all-to-all(f32[8,1,9,256]{3,1,2,0:T(1,128)S(1)} %stack.12), channel_id=1, replica_groups=mesh['obs_0'=8,'obs_1'=4,'obs_2'=2,'rep'=4] {'obs_0'}, dimensions={0} | all-to-all | bytes 147456 | tf_op jit(solution)/shard_map/all_to_all | solution.py:51
  260.6 5.7 %all-to-all-done.4 = f32[4,8,9,256]{3,1,2,0:T(8,128)S(1)} async-done(((f32[4,8,9,256]{3,1,2,0:T(8,128)}), f32[4,8,9,256]{3,1,2,0:T(8,128)S(1)}, u32[]{:S(2)}, u32[]{:S(2)}) %all-to-all-start.4) | async-done | bytes 294944 | tf_op jit(solution)/shard_map/all_to_all | solution.py:51
  270.7 6.0 %all-to-all-done.7 = f32[4,81,256]{2,1,0:T(8,128)S(1)} async-done(((f32[4,81,256]{2,1,0:T(8,128)}), f32[4,81,256]{2,1,0:T(8,128)S(1)}, u32[]{:S(2)}, u32[]{:S(2)}) %all-to-all-start.7) | async-done | bytes 331808 | tf_op jit(solution)/shard_map/all_to_all | solution.py:65
  282.4 11.0 %all-to-all-done.5 = f32[4,32,9,256]{3,1,2,0:T(8,128)S(1)} async-done(((f32[4,32,9,256]{3,1,2,0:T(8,128)}), f32[4,32,9,256]{3,1,2,0:T(8,128)S(1)}, u32[]{:S(2)}, u32[]{:S(2)}) %all-to-all-start.5) | async-done | bytes 1179680 | tf_op jit(solution)/shard_map/all_to_all | solution.py:51
  293.8 10.7 %all_to_all.42 = f32[2,128,9,256]{3,1,2,0:T(8,128)S(1)} all-to-all(f32[2,128,9,256]{3,1,2,0:T(8,128)S(1)} %pad_maximum_fusion.1), channel_id=1, replica_groups=mesh['obs_0'=8,'obs_1'=4,'obs_2'=2,'rep'=4] {'obs_2'}, dimensions={0} | all-to-all | bytes 4718592 | tf_op jit(solution)/shard_map/all_to_all | solution.py:51
  310.1 16.8 %copy.57 = f32[9,256,256]{0,2,1:T(8,128)} copy(f32[9,256,256]{2,1,0:T(8,128)S(1)} %bitcast.49) | data formatting | bytes 4718592 | tf_op jit(solution)/shard_map/reshape | solution.py:44
  326.9 172.8 %scatter_custom_fusion = f32[9,65536]{0,1:T(8,128)} fusion(s32[65536]{0:T(1024)S(1)} %compare_select_fusion, f32[65536,9]{1,0:T(8,128)} %bitcast.45, f32[]{:T(128)} %constant.34.clone.1), kind=kCustom, calls=%fused_computation.14 | custom fusion | bytes 2359808 | tf_op jit(solution)/shard_map/scatter | solution.py:140
  499.6 19.4 %copy.56 = f32[9,65536]{1,0:T(8,128)} copy(f32[9,65536]{0,1:T(8,128)} %scatter_custom_fusion) | data formatting | bytes 4718592
  (247 shorter events, 109.9 us)
Async XLA Ops:
  3.2 24.8 %all-to-all-start.1 = ((s32[1,64,513]{2,0,1:T(1,128)}), s32[1,64,513]{2,0,1:T(1,128)S(1)}, u32[]{:S(2)}, u32[]{:S(2)}) async-start(s32[1,64,513]{2,0,1:T(1,128)} %copy.48), calls=%async_computation.1 | async-start | bytes 327680 | tf_op jit(solution)/shard_map/all_to_all | solution.py:16
  28.0 7.0 %copy-start = (s32[1,64,513]{2,0,1:T(1,128)}, s32[1,64,513]{2,0,1:T(1,128)S(1)}, u32[]{:S(2)}) copy-start(s32[1,64,513]{2,0,1:T(1,128)S(1)} %all-to-all-done.1) | copy-start | bytes 393988
  28.0 79.4 %all-to-all-start = ((f32[20,64,512]{2,0,1:T(8,128)}), f32[20,64,512]{2,0,1:T(8,128)S(1)}, u32[]{:S(2)}, u32[]{:S(2)}) async-start(f32[20,64,512]{2,0,1:T(8,128)} %copy.45), calls=%async_computation | async-start | bytes 6291456 | tf_op jit(solution)/shard_map/all_to_all | solution.py:16
  109.1 3.6 slice-start
  112.8 2.1 copy-start.1
  120.2 2.1 copy-start.1
  127.5 2.1 copy-start.1
  134.9 2.1 copy-start.1
  142.3 2.1 copy-start.1
  149.7 2.1 copy-start.1
  157.0 2.1 copy-start.1
  164.4 2.1 copy-start.1
  171.8 2.1 copy-start.1
  179.2 2.1 copy-start.1
  186.5 2.1 copy-start.1
  193.9 2.1 copy-start.1
  201.3 2.1 copy-start.1
  208.7 2.1 copy-start.1
  216.1 2.1 copy-start.1
  223.4 2.1 copy-start.1
  257.2 9.1 %all-to-all-start.4 = ((f32[4,8,9,256]{3,1,2,0:T(8,128)}), f32[4,8,9,256]{3,1,2,0:T(8,128)S(1)}, u32[]{:S(2)}, u32[]{:S(2)}) async-start(f32[4,8,9,256]{3,1,2,0:T(8,128)} %stack.13), calls=%async_computation.4 | async-start | bytes 589824 | tf_op jit(solution)/shard_map/all_to_all | solution.py:51
  267.1 14.3 %copy-start.4 = (s32[65536]{0:T(1024)S(1)}, s32[65536]{0:T(1024)}, u32[]{:S(2)}) copy-start(s32[65536]{0:T(1024)} %param.11) | copy-start | bytes 786436
  267.1 9.6 %all-to-all-start.7 = ((f32[4,81,256]{2,1,0:T(8,128)}), f32[4,81,256]{2,1,0:T(8,128)S(1)}, u32[]{:S(2)}, u32[]{:S(2)}) async-start(f32[4,81,256]{2,1,0:T(8,128)} %broadcast_in_dim.36), calls=%async_computation.7 | async-start | bytes 720896 | tf_op jit(solution)/shard_map/all_to_all | solution.py:65
  277.8 15.6 %all-to-all-start.5 = ((f32[4,32,9,256]{3,1,2,0:T(8,128)}), f32[4,32,9,256]{3,1,2,0:T(8,128)S(1)}, u32[]{:S(2)}, u32[]{:S(2)}) async-start(f32[4,32,9,256]{3,1,2,0:T(8,128)} %stack.14), calls=%async_computation.5 | async-start | bytes 2359296 | tf_op jit(solution)/shard_map/all_to_all | solution.py:51
  (17 other events, 12.8 us)
